TPU v7x, 32 devices: a whole 2x2x4 slice. The times are simulated.
32 devices in a mesh: samp: 16 (over z, y, x), tile: 2 (over core).
Axes of the slice: x: 2, y: 2, z: 4, core: 2. Of those that a mesh axis runs over, the one named last changes fastest.
Arguments:
- traits: bfloat16 [16384, 1024], P('samp'), may hold values from -300 to 300
- covariates: bfloat16 [16384, 32], P('samp'), may hold values from -6 to 6
- genotypes: int32 [16384, 512], P('samp', 'tile'), may hold values from 0 to 2
- shuffles: int32 [6, 16384], P(None, 'samp'), may hold values from 0 to 16383, as said below
Outputs:
- observed: float32 [1024, 512], P('samp', 'tile')
- perm_max: float32 [6, 1024], P(None, 'samp')
Inputs may be any that keep to these rules, and one draw needn't show every extreme that they name: Row p of shuffles maps each aligned block of 1024 samples one to one onto the same block's samples.
All inputs are finite; a program needn't handle non-finite values.
Results may differ from a plain program's by a relative error of at most 0.0045.
Values sent between devices are 32-bit elements; how exact they have to be, the bound alone decides.
A program may use at most 64 MiB of HBM per device.

v0:
```python
import functools
import math

import jax
import jax.numpy as jnp
from jax import lax
from jax.experimental import pallas as pl
from jax.experimental.pallas import tpu as pltpu
from jax.sharding import PartitionSpec as P

MESH = pl.DeviceIdType.MESH
LANES = 128
F32, BF16 = jnp.float32, jnp.bfloat16
epsilon = 1e-05

def parts_of(own, width):
    cut, half = own - max(8, own // 64 * 8), width // 2
    return (
        ((2, 1, 0), slice(0, cut), slice(0, half)),
        ((1, 2, 0), slice(0, cut), slice(half, width)),
        ((0, 2, 1), slice(cut, own), slice(0, width)),
    )


def grid_of(groups):
    x = 4 if groups % 32 == 0 else 2
    y = 2
    return (groups // (x * y), y, x)


def start_all(copies):
    for copy in copies:
        copy.start()
    return copies


def scan_kernel(
    dims, tiles, samples, used, areas, t_ref, c_ref, g_ref, order_ref, score_ref, peak_ref,
    design, parts, landed, mine, full, rhs, coef, rt, rg, moved, found, squares, column,
    peaks, sum_sems, sq_send, sq_recv, tile_send, tile_recv, send, recv, *bufs
):
    groups = dims[0] * dims[1] * dims[2]
    me = lax.axis_index("samp")
    my_tile = lax.axis_index("tile")
    here = (me // (dims[1] * dims[2]), lax.rem(me // dims[2], dims[1]), lax.rem(me, dims[2]))
    turns, width, n_parts = found.shape[0], found.shape[2], len(areas)
    local, traits = t_ref.shape
    own = traits // groups
    rows = coef.shape[0]
    quota = parts.shape[0] // groups

    barrier = pltpu.get_barrier_semaphore()
    for d in range(1, groups):
        pl.semaphore_signal(
            barrier, inc=1, device_id={"samp": lax.rem(me + d, groups)}, device_id_type=MESH
        )
    for d in range(1, tiles):
        pl.semaphore_signal(
            barrier, inc=1, device_id={"tile": lax.rem(my_tile + d, tiles)}, device_id_type=MESH
        )

    lane = lax.broadcasted_iota(jnp.int32, design.shape, 1)
    design[...] = jnp.where(lane == used - 1, 1.0, 0.0).astype(BF16)
    design[:, : used - 1] = c_ref[...]
    strips = -(-used // 8)
    design_t = design[...].T[: -(-used // 16) * 16]
    slot = 0
    for block_ref in (t_ref, g_ref, design):
        block = block_ref[...]
        if block.dtype != BF16:
            block = block.astype(F32).astype(BF16)
        block = jnp.dot(design_t, block, preferred_element_type=F32)
        for c in range(block.shape[1] // LANES):
            for r in range(strips):
                parts[slot] = block[8 * r : 8 * r + 8, LANES * c : LANES * c + LANES]
                slot += 1
    for i in range(slot, parts.shape[0]):
        parts[i] = jnp.zeros((8, LANES), F32)
    pl.semaphore_wait(barrier, groups + tiles - 2)

    def sum_copy(d, source, target, stage):
        return pltpu.make_async_remote_copy(
            src_ref=source,
            dst_ref=target,
            send_sem=sum_sems.at[2 * stage, d - 1],
            recv_sem=sum_sems.at[2 * stage + 1, d - 1],
            device_id={"samp": lax.rem(me + d, groups)},
            device_id_type=MESH,
        )

    scattered = start_all(
        [
            sum_copy(
                d, parts.at[pl.ds(lax.rem(me + d, groups) * quota, quota)], landed.at[d - 1], 0
            )
            for d in range(1, groups)
        ]
    )
    total = parts[pl.ds(me * quota, quota)]
    for d in range(1, groups):
        scattered[d - 1].wait_recv()
        total = total + landed[d - 1]
    mine[...] = total
    full[pl.ds(me * quota, quota)] = total
    gathered = start_all(
        [sum_copy(d, mine, full.at[pl.ds(me * quota, quota)], 1) for d in range(1, groups)]
    )
    rhs[...] = jnp.zeros(rhs.shape, F32)
    for copy in gathered:
        copy.wait_recv()

    n_t, n_g = traits // LANES, width // LANES
    half = rows // 2
    for c in range(n_t + n_g):
        for r in range(strips):
            rhs[half + 8 * r : half + 8 * r + 8, LANES * c : LANES * c + LANES] = full[
                c * strips + r
            ]
    gram = jnp.concatenate([full[(n_t + n_g) * strips + r] for r in range(strips)], axis=0)
    sub = lax.broadcasted_iota(jnp.int32, gram.shape, 0)
    lane = lax.broadcasted_iota(jnp.int32, gram.shape, 1)
    gram = jnp.where(lane == sub + half, 1.0, gram)
    for j in range(used):
        row = gram[j : j + 1, :] * (1.0 / gram[j : j + 1, j : j + 1])
        gram = jnp.where(sub == j, row, gram - gram[:, j : j + 1] * row)
    inverse = jnp.where(lane >= half, gram, 0.0)
    coef[...] = jnp.zeros(coef.shape, BF16)
    coef[: 8 * strips, :] = jnp.dot(
        inverse, rhs[...], precision=lax.Precision.HIGHEST, preferred_element_type=F32
    ).astype(BF16)

    step = min(256, local)
    sq_t = jnp.zeros((1, traits), F32)
    sq_g = jnp.zeros((1, width), F32)
    for i in range(local // step):
        at = slice(i * step, (i + 1) * step)
        d = design[at, :]
        resid = t_ref[at, :].astype(F32) - jnp.dot(
            d, coef[:, :traits], preferred_element_type=F32
        )
        sq_t = sq_t + jnp.sum(resid * resid, axis=0, keepdims=True)
        rt[:, at] = resid.astype(BF16).T
        dose = g_ref[at, :].astype(F32)
        resid = dose - jnp.dot(d, coef[:, traits:], preferred_element_type=F32)
        sq_g = sq_g + jnp.sum(resid * resid, axis=0, keepdims=True)
        rg[at, :] = resid.astype(BF16)
    squares[0] = jnp.zeros(squares.shape[1:], F32)
    for c in range(n_t):
        squares[0, c : c + 1, :] = sq_t[:, c * LANES : (c + 1) * LANES]
    for c in range(n_g):
        squares[0, n_t + c : n_t + c + 1, :] = sq_g[:, c * LANES : (c + 1) * LANES]

    def square_copy(d):
        return pltpu.make_async_remote_copy(
            src_ref=squares.at[0],
            dst_ref=squares.at[d],
            send_sem=sq_send.at[d - 1],
            recv_sem=sq_recv.at[d - 1],
            device_id={"samp": lax.rem(me + d, groups)},
            device_id_type=MESH,
        )

    def spot(axis, d):
        j = lax.rem(here[axis] + d, dims[axis])
        at = list(here)
        at[axis] = j
        return j, (at[0] * dims[1] + at[1]) * dims[2] + at[2]

    def pick(axis, order, stage, j):
        left = [a for a in (0, 1, 2) if a not in order[:stage]]
        return tuple(j if a == axis else slice(None) for a in left)

    def source(k, p, stage):
        return bufs[6 * p + 2 * stage].at[k]

    def copies(k, p, stage):
        order = areas[p][0]
        axis = order[stage]
        first = sum(dims[a] - 1 for a in order[:stage])
        out = []
        for d in range(1, dims[axis]):
            j, peer = spot(axis, d)
            out.append(
                pltpu.make_async_remote_copy(
                    src_ref=source(k, p, stage).at[pick(axis, order, stage, j)],
                    dst_ref=bufs[6 * p + 2 * stage + 1].at[k, d - 1],
                    send_sem=send.at[k, p, first + d - 1],
                    recv_sem=recv.at[k, p, first + d - 1],
                    device_id={"samp": peer},
                    device_id_type=MESH,
                )
            )
        return out

    def begin(k, stage):
        for p in range(n_parts):
            for copy in copies(k, p, stage):
                copy.start()

    def collect(k, stage):
        for p in range(n_parts):
            order = areas[p][0]
            axis = order[stage]
            for copy in copies(k, p, stage):
                copy.wait_recv()
            total = source(k, p, stage)[pick(axis, order, stage, here[axis])]
            for d in range(1, dims[axis]):
                total = total + bufs[6 * p + 2 * stage + 1][k, d - 1]
            if stage < 2:
                bufs[6 * p + 2 * stage + 2][k] = total
            else:
                found[k, areas[p][1], areas[p][2]] = total

    def multiply(k):
        @pl.when(k == 0)
        def _():
            moved[...] = rg[...]

        @pl.when(k > 0)
        def _():
            order = order_ref[pl.ds(k - 1, 1), :] - me * local
            for i in range(local // step):
                row = lax.broadcasted_iota(jnp.int32, (step, local), 0) + i * step
                hot = jnp.where(row == order, 1.0, 0.0).astype(BF16)
                moved[i * step : (i + 1) * step, :] = jnp.dot(
                    hot, rg[...], preferred_element_type=F32
                ).astype(BF16)

        depth = traits // dims[0]
        for z in range(dims[0]):
            block = jnp.dot(
                rt[z * depth : (z + 1) * depth, :], moved[...], preferred_element_type=F32
            ).reshape(dims[1], dims[2], own, width)
            for p in range(n_parts):
                bufs[6 * p][k, z] = block[:, :, areas[p][1], areas[p][2]]

    def turn(t, carry):
        @pl.when(t < turns)
        def _():
            multiply(t)
            begin(t, 0)

        @pl.when(t == 0)
        def _():
            for d in range(1, groups):
                square_copy(d).start()

        for stage in range(3):
            k = t - 1 - stage

            @pl.when(jnp.logical_and(k >= 0, k < turns))
            def _():
                collect(k, stage)
                if stage < 2:
                    begin(k, stage + 1)

        return carry

    lax.fori_loop(0, turns + 3, turn, 0)

    total = squares[0]
    for d in range(1, groups):
        square_copy(d).wait_recv()
        total = total + squares[d]
    gain = lax.rsqrt(total / samples + epsilon)
    factor = math.sqrt(samples - used - 1) / samples
    gain_g = jnp.concatenate([gain[n_t + c : n_t + c + 1, :] for c in range(n_g)], axis=1)
    turned = gain.T
    pos = lax.broadcasted_iota(jnp.int32, turned.shape, 1)
    chosen = jnp.sum(
        jnp.where(pos == me * own // LANES, turned, 0.0), axis=1, keepdims=True
    )
    column[...] = jnp.broadcast_to(chosen * factor, column.shape)
    gain_t = column[pl.ds(pl.multiple_of(lax.rem(me * own, LANES), 8), own), :]
    gain_t = gain_t[:, :1]
    score_ref[...] = found[0] * gain_g * gain_t
    top = jnp.zeros((own, LANES), F32)
    pos = lax.broadcasted_iota(jnp.int32, top.shape, 1)
    for k in range(1, turns):
        peak = jnp.max(jnp.abs(found[k] * gain_g), axis=1, keepdims=True) * gain_t
        top = jnp.where(pos == k - 1, peak, top)
    peaks[0] = top
    crossed = start_all(
        [
            pltpu.make_async_remote_copy(
                src_ref=peaks.at[0],
                dst_ref=peaks.at[d],
                send_sem=tile_send.at[d - 1],
                recv_sem=tile_recv.at[d - 1],
                device_id={"tile": lax.rem(my_tile + d, tiles)},
                device_id_type=MESH,
            )
            for d in range(1, tiles)
        ]
    )
    for copy in scattered + gathered:
        copy.wait_send()

    def finish(k, carry):
        for p in range(n_parts):
            for stage in range(3):
                for copy in copies(k, p, stage):
                    copy.wait_send()
        return carry

    lax.fori_loop(0, turns, finish, 0)
    for d in range(1, groups):
        square_copy(d).wait_send()
    for d in range(1, tiles):
        crossed[d - 1].wait()
        top = jnp.maximum(top, peaks[d])
    peak_ref[...] = top.T[: turns - 1]


def scan(traits, covariates, genotypes, shuffles):
    groups, tiles = lax.axis_size("samp"), lax.axis_size("tile")
    dims = grid_of(groups)
    turns = shuffles.shape[0] + 1
    local, n_traits = traits.shape
    width = genotypes.shape[1]
    used = covariates.shape[1] + 1
    own = n_traits // groups
    areas = parts_of(own, width)
    n_parts = len(areas)
    bufs = []
    for order, part_rows, part_lanes in areas:
        size = (part_rows.stop - part_rows.start, part_lanes.stop - part_lanes.start)
        left = [0, 1, 2]
        bufs.append(pltpu.VMEM((turns,) + dims + size, F32))
        for stage, axis in enumerate(order):
            left.remove(axis)
            rest = tuple(dims[a] for a in left) + size
            bufs.append(pltpu.VMEM((turns, dims[axis] - 1) + rest, F32))
            if stage < 2:
                bufs.append(pltpu.VMEM((turns,) + rest, F32))
    hops = sum(n - 1 for n in dims)
    rows = -(-(n_traits + width) // (8 * LANES)) * 8
    strips = -(-used // 8)
    quota = -(-strips * ((n_traits + width) // LANES + 1) // groups)
    vmem = pl.BlockSpec(memory_space=pltpu.VMEM)
    sems = pltpu.SemaphoreType.DMA((turns, n_parts, hops))
    flat = pltpu.SemaphoreType.DMA((groups - 1,))
    pair = pltpu.SemaphoreType.DMA((max(tiles - 1, 1),))
    return pl.pallas_call(
        functools.partial(scan_kernel, dims, tiles, local * groups, used, areas),
        out_shape=(
            jax.ShapeDtypeStruct((own, width), F32),
            jax.ShapeDtypeStruct((turns - 1, own), F32),
        ),
        in_specs=[vmem] * 4,
        out_specs=(vmem, vmem),
        scratch_shapes=[
            pltpu.VMEM((local, LANES), BF16),
            pltpu.VMEM((quota * groups, 8, LANES), F32),
            pltpu.VMEM((groups - 1, quota, 8, LANES), F32),
            pltpu.VMEM((quota, 8, LANES), F32),
            pltpu.VMEM((quota * groups, 8, LANES), F32),
            pltpu.VMEM((LANES, n_traits + width), F32),
            pltpu.VMEM((LANES, n_traits + width), BF16),
            pltpu.VMEM((n_traits, local), BF16),
            pltpu.VMEM((local, width), BF16),
            pltpu.VMEM((local, width), BF16),
            pltpu.VMEM((turns, own, width), F32),
            pltpu.VMEM((groups, rows, LANES), F32),
            pltpu.VMEM((LANES, LANES), F32),
            pltpu.VMEM((tiles, own, LANES), F32),
            pltpu.SemaphoreType.DMA((4, groups - 1)),
            flat,
            flat,
            pair,
            pair,
            sems,
            sems,
            *bufs,
        ],
        compiler_params=pltpu.CompilerParams(
            collective_id=0, has_side_effects=True, vmem_limit_bytes=60 * 1024 * 1024
        ),
        name="scan",
    )(traits, covariates, genotypes, shuffles)


def shards(traits, covariates, genotypes, shuffles):
    return scan(traits, covariates, genotypes, shuffles)


def solution(mesh):
    placed = (P("samp", None), P("samp", None), P("samp", "tile"), P(None, "samp"))
    return jax.shard_map(
        shards,
        mesh=mesh,
        in_specs=placed,
        out_specs=(P("samp", "tile"), P(None, "samp")),
        check_vma=False,
    )
```

profile of v0, /device:TPU:0, one launch (start us, length us, event | category | flops | bytes accessed | tf_op | source)
XLA Modules:
  0.0 100.7 jit_solution(13379347590834996139)
XLA Ops:
  0.6 1.7 %copy.6.c_ref = bf16[1024,32]{1,0:T(8,128)(2,1)} copy(bf16[1024,32]{0,1:T(8,128)(2,1)} %param.5) | data formatting | bytes 131072 | tf_op args[1]
  2.3 95.6 %scan.1 = (f32[64,256]{1,0:T(8,128)}, f32[6,64]{1,0:T(8,128)}) custom-call(bf16[1024,1024]{1,0:T(8,128)(2,1)} %t_ref.1, bf16[1024,32]{1,0:T(8,128)(2,1)} %copy.6.c_ref, s32[1024,256]{1,0:T(8,128)} %g_ref.1, s32[6,1024]{1,0:T(8,128)} %order_ref.1), custom_call_target="tpu_custom_call" | custom-call | tf_op jit(solution)/shard_map/scan/pallas_call | solution.py:344
  98.0 1.5 %copy.9 = f32[64,256]{1,0:T(8,128)} copy(f32[64,256]{1,0:T(8,128)} %get-tuple-element.4) | data formatting | bytes 131072
  99.4 1.3 %copy.10 = f32[6,64]{1,0:T(8,128)} copy(f32[6,64]{1,0:T(8,128)} %get-tuple-element.5) | data formatting | bytes 3072
where the time goes:
time: 101 us
  Pallas kernels  95.6 us (95%)
  local copies, waits for them, and re-layouts  4.42 us (4%)
    pallas_call x1, Pallas kernels, scan(): pl.pallas_call(functools.partial(scan_kernel, dims, tiles, local * groups...  95.6 us
    unnamed x3, local copies, waits for them, and re-layouts  4.42 us

commit v1 on v0

v1 whole, which is shorter than its diff:
```python
import functools
import math

import jax
import jax.numpy as jnp
from jax import lax
from jax.experimental import pallas as pl
from jax.experimental.pallas import tpu as pltpu
from jax.sharding import PartitionSpec as P

MESH = pl.DeviceIdType.MESH
LANES = 128
F32, BF16 = jnp.float32, jnp.bfloat16
HIGHEST = lax.Precision.HIGHEST
epsilon = 1e-05


def parts_of(bits, own, width):
    cut, half = own - max(8, own // 32 * 8), width // 2
    low, high, rest = tuple(range(2)), tuple(range(2, bits)), tuple(range(3, bits))
    return (
        ((0, 1) + high, slice(0, cut), slice(0, half)),
        ((1, 0) + high, slice(0, cut), slice(half, width)),
        (high + low, slice(cut, own), slice(0, half)),
        ((2, 1, 0) + rest, slice(cut, own), slice(half, width)),
    )


def place_of(order, g):
    at = [(g >> bit) & 1 for bit in order]
    rest = 0
    for bit in at[1:]:
        rest = 2 * rest + bit
    return at[0], rest


def scan_kernel(
    groups, tiles, samples, used, areas, t_hbm, c_hbm, g_hbm, order_hbm, score_ref, peak_ref,
    t_ref, c_ref, g_ref, order_ref, load, design, parts, landed, mine, full, rhs, coef, rt, rg,
    moved, found, fix, gram_ref, notes, squares, column, peaks, sum_sems, sq_send, sq_recv,
    tile_send, tile_recv, send, recv, *bufs
):
    me = lax.axis_index("samp")
    my_tile = lax.axis_index("tile")
    turns, width, n_parts = found.shape[0], found.shape[2], len(areas)
    bits = len(areas[0][0])
    local, traits = t_ref.shape
    own = traits // groups
    share = traits // tiles
    quota = parts.shape[0] // groups

    def samp_peer(d):
        return {"samp": lax.rem(me + d, groups)}

    def tile_peer(d):
        return {"tile": lax.rem(my_tile + d, tiles)}

    barrier = pltpu.get_barrier_semaphore()
    for d in range(1, groups):
        pl.semaphore_signal(barrier, inc=1, device_id=samp_peer(d), device_id_type=MESH)
    for d in range(1, tiles):
        pl.semaphore_signal(barrier, inc=1, device_id=tile_peer(d), device_id_type=MESH)
    loads = [
        pltpu.make_async_copy(a, b, load.at[i])
        for i, (a, b) in enumerate(
            ((c_hbm, c_ref), (t_hbm, t_ref), (g_hbm, g_ref), (order_hbm, order_ref))
        )
    ]
    for copy in loads:
        copy.start()
    for copy in loads:
        copy.wait()

    lane = lax.broadcasted_iota(jnp.int32, (LANES - used + 1, local), 0)
    design_t = jnp.concatenate(
        [c_ref[...].astype(F32), jnp.where(lane == 0, 1.0, 0.0)], axis=0
    )
    design[...] = design_t.T.astype(BF16)
    design_t = design_t[: -(-used // 16) * 16].astype(BF16)
    n_t, n_g = share // LANES, width // LANES
    n_blocks = n_t + n_g + 1
    whole, rest = used // 8, used % 8
    strips = -(-used // 8)

    def spot(c, r):
        at = c * rest + r
        return n_blocks * whole + at // 8, at % 8

    for i in range(n_blocks * whole, parts.shape[0]):
        parts[i] = jnp.zeros((8, LANES), F32)
    dose = g_ref[...].astype(F32)
    first = 0
    for block in (
        t_ref[:, pl.ds(pl.multiple_of(my_tile * share, LANES), share)],
        dose.astype(BF16),
        design[...],
    ):
        block = jnp.dot(design_t, block, preferred_element_type=F32)
        for c in range(block.shape[1] // LANES):
            at = slice(LANES * c, LANES * c + LANES)
            for r in range(whole):
                parts[(first + c) * whole + r] = block[8 * r : 8 * r + 8, at]
            for r in range(rest):
                slot, row = spot(first + c, r)
                parts[slot, row : row + 1, :] = block[8 * whole + r : 8 * whole + r + 1, at]
        first += block.shape[1] // LANES

    def source(p, stage):
        return bufs[2 * p * bits + 2 * stage]

    def target(p, stage):
        return bufs[2 * p * bits + 2 * stage + 1]

    def side(p, stage):
        bit = areas[p][0][stage]
        return lax.rem(me // 2**bit, 2), 2**bit

    def copies(k, stage):
        out = []
        for p in range(n_parts):
            b, far = side(p, stage)
            out.append(
                pltpu.make_async_remote_copy(
                    src_ref=source(p, stage).at[k, 1 - b],
                    dst_ref=target(p, stage).at[k],
                    send_sem=send.at[k, p, stage],
                    recv_sem=recv.at[k, p, stage],
                    device_id={"samp": me + (1 - 2 * b) * far},
                    device_id_type=MESH,
                )
            )
        return out

    def begin(k, stage):
        for copy in copies(k, stage):
            copy.start()

    def collect(k, stage):
        for copy in copies(k, stage):
            copy.wait_recv()
        for p in range(n_parts):
            b, _ = side(p, stage)
            total = source(p, stage)[k, b] + target(p, stage)[k]
            if stage < bits - 1:
                source(p, stage + 1)[k] = total.reshape(source(p, stage + 1).shape[1:])
            else:
                found[k, areas[p][1], areas[p][2]] = total[0]

    def cross(k, right):
        batch = max(groups // 4, 1)
        for q in range(groups // batch):
            rows = batch * own
            block = jnp.dot(
                rt[q * rows : (q + 1) * rows, :], right, preferred_element_type=F32
            )
            for i in range(batch):
                for p in range(n_parts):
                    order, part_rows, part_lanes = areas[p]
                    lead, other = place_of(order, q * batch + i)
                    source(p, 0)[k, lead, other] = block[i * own : (i + 1) * own][
                        part_rows, part_lanes
                    ]

    step = min(256, local)
    for i in range(local // step):
        at = slice(i * step, (i + 1) * step)
        rt[:, at] = t_ref[at, :].T
    cross(0, (dose - 1.0).astype(BF16))
    pl.semaphore_wait(barrier, groups + tiles - 2)

    def sum_copy(d, source, target, stage):
        return pltpu.make_async_remote_copy(
            src_ref=source,
            dst_ref=target,
            send_sem=sum_sems.at[2 * stage, d - 1],
            recv_sem=sum_sems.at[2 * stage + 1, d - 1],
            device_id=samp_peer(d),
            device_id_type=MESH,
        )

    scattered = [
        sum_copy(d, parts.at[pl.ds(lax.rem(me + d, groups) * quota, quota)], landed.at[d - 1], 0)
        for d in range(1, groups)
    ]
    for copy in scattered:
        copy.start()
    begin(0, 0)
    total = parts[pl.ds(me * quota, quota)]
    for d in range(1, groups):
        scattered[d - 1].wait_recv()
        total = total + landed[d - 1]
    mine[...] = total
    full[my_tile, pl.ds(me * quota, quota)] = total
    gathered = [
        sum_copy(d, mine, full.at[my_tile, pl.ds(me * quota, quota)], 1)
        for d in range(1, groups)
    ]
    for copy in gathered:
        copy.start()
    rhs[...] = jnp.zeros(rhs.shape, F32)
    gram_ref[...] = jnp.zeros(gram_ref.shape, F32)
    coef[...] = jnp.zeros(coef.shape, BF16)
    collect(0, 0)
    begin(0, 1)
    for copy in gathered:
        copy.wait_recv()

    def spread_copy(d):
        return pltpu.make_async_remote_copy(
            src_ref=full.at[my_tile],
            dst_ref=full.at[my_tile],
            send_sem=tile_send.at[tiles - 1 + d - 1],
            recv_sem=tile_recv.at[tiles - 1 + d - 1],
            device_id=tile_peer(d),
            device_id_type=MESH,
        )

    spread = [spread_copy(d) for d in range(1, tiles)]
    for copy in spread:
        copy.start()
    collect(0, 1)
    begin(0, 2)

    half = LANES // 2
    last = n_blocks - 1
    for r in range(whole):
        gram_ref[8 * r : 8 * r + 8, :] = full[my_tile, last * whole + r]
    for r in range(rest):
        slot, row = spot(last, r)
        gram_ref[8 * whole + r : 8 * whole + r + 1, :] = full[my_tile, slot, row : row + 1, :]
    gram = gram_ref[: 8 * strips, :]
    sub = lax.broadcasted_iota(jnp.int32, gram.shape, 0)
    lane = lax.broadcasted_iota(jnp.int32, gram.shape, 1)
    gram = jnp.where(lane == sub + half, 1.0, gram)
    for j in range(used):
        row = gram[j : j + 1, :] * (1.0 / gram[j : j + 1, j : j + 1])
        gram = jnp.where(sub == j, row, gram - gram[:, j : j + 1] * row)
    inverse = jnp.where(lane >= half, gram, 0.0)
    for copy in spread:
        copy.wait_recv()
    for tile in range(tiles + 1):
        held = full.at[tile] if tile < tiles else full.at[my_tile]
        for c in range(n_t if tile < tiles else n_g):
            block = c + (0 if tile < tiles else n_t)
            at = LANES * (tile * n_t + c)
            for r in range(whole):
                rhs[half + 8 * r : half + 8 * r + 8, at : at + LANES] = held[block * whole + r]
            for r in range(rest):
                slot, row = spot(block, r)
                to = half + 8 * whole + r
                rhs[to : to + 1, at : at + LANES] = held[slot, row : row + 1, :]
    coef[: 8 * strips, :] = jnp.dot(
        inverse, rhs[...], precision=HIGHEST, preferred_element_type=F32
    ).astype(BF16)
    collect(0, 2)
    begin(0, 3)

    sq_t = jnp.zeros((1, traits), F32)
    sq_g = jnp.zeros((1, width), F32)
    for i in range(local // step):
        at = slice(i * step, (i + 1) * step)
        d = design[at, :]
        resid = t_ref[at, :].astype(F32) - jnp.dot(
            d, coef[:, :traits], preferred_element_type=F32
        )
        sq_t = sq_t + jnp.sum(resid * resid, axis=0, keepdims=True)
        rt[:, at] = resid.astype(BF16).T
        dose = g_ref[at, :].astype(F32)
        resid = dose - jnp.dot(d, coef[:, traits:], preferred_element_type=F32)
        sq_g = sq_g + jnp.sum(resid * resid, axis=0, keepdims=True)
        rg[at, :] = resid.astype(BF16)

    def note_squares():
        for j in range(groups):
            at = j * own // LANES * LANES
            notes[j, 0:1, :] = sq_t[:, at : at + LANES]
            for c in range(n_g):
                notes[j, 1 + c : 2 + c, :] = sq_g[:, c * LANES : (c + 1) * LANES]
            if n_g < 7:
                notes[j, 1 + n_g :, :] = jnp.zeros((7 - n_g, LANES), F32)

    def square_copy(d):
        return pltpu.make_async_remote_copy(
            src_ref=notes.at[lax.rem(me + d, groups)],
            dst_ref=squares.at[d],
            send_sem=sq_send.at[d - 1],
            recv_sem=sq_recv.at[d - 1],
            device_id=samp_peer(d),
            device_id_type=MESH,
        )

    note_squares()
    squares[0] = notes[me]

    def permute(k):
        order = order_ref[pl.ds(k - 1, 1), :] - me * local
        for i in range(local // step):
            row = lax.broadcasted_iota(jnp.int32, (step, local), 0) + i * step
            hot = jnp.where(row == order, 1.0, 0.0).astype(BF16)
            moved[i * step : (i + 1) * step, :] = jnp.dot(
                hot, rg[...], preferred_element_type=F32
            ).astype(BF16)

    lead = pl.multiple_of(me * own // LANES * LANES, LANES)
    shift = pl.multiple_of(lax.rem(me * own, LANES), 8)

    def correct():
        gram = gram_ref[...]
        lane = lax.broadcasted_iota(jnp.int32, gram.shape, 1)
        gram = jnp.where(lane < half, gram, 0.0)
        coef_g = coef[:, traits:].astype(F32)
        miss = rhs[half:, traits:] - jnp.dot(
            gram, coef_g, precision=HIGHEST, preferred_element_type=F32
        )
        sub = lax.broadcasted_iota(jnp.int32, (half, width), 0)
        fit = coef_g[:half] - jnp.where(sub == used - 1, 1.0, 0.0)
        left = jnp.concatenate(
            [rhs[half:, pl.ds(lead, LANES)], coef[:half, pl.ds(lead, LANES)].astype(F32)], axis=0
        )
        column[...] = left.T
        fix[...] = jnp.dot(
            column[pl.ds(shift, own), :],
            jnp.concatenate([fit, miss], axis=0),
            precision=HIGHEST,
            preferred_element_type=F32,
        )

    def turn(t, carry):
        @pl.when(t < turns)
        def _():
            permute(t)
            cross(t, moved[...])
            begin(t, 0)

        @pl.when(t == 1)
        def _():
            for d in range(1, groups):
                square_copy(d).start()
            correct()

        for stage in range(bits):
            k = t - 1 - stage

            @pl.when(jnp.logical_and(k >= (0 if stage > 2 else 1), k < turns))
            def _():
                collect(k, stage)
                if stage < bits - 1:
                    begin(k, stage + 1)

        return carry

    lax.fori_loop(1, turns + bits, turn, 0)

    total = squares[0]
    for d in range(1, groups):
        square_copy(d).wait_recv()
        total = total + squares[d]
    gain = lax.rsqrt(total / samples + epsilon)
    factor = math.sqrt(samples - used - 1) / samples
    gain_g = jnp.concatenate([gain[1 + c : 2 + c, :] for c in range(n_g)], axis=1)
    column[...] = jnp.broadcast_to(gain.T[:, :1] * factor, column.shape)
    gain_t = column[pl.ds(shift, own), :]
    gain_t = gain_t[:, :1]
    score_ref[...] = (found[0] - fix[...]) * gain_g * gain_t
    top = jnp.zeros((own, LANES), F32)
    pos = lax.broadcasted_iota(jnp.int32, top.shape, 1)
    for k in range(1, turns):
        peak = jnp.max(jnp.abs(found[k] * gain_g), axis=1, keepdims=True) * gain_t
        top = jnp.where(pos == k - 1, peak, top)
    peaks[0] = top
    crossed = [
        pltpu.make_async_remote_copy(
            src_ref=peaks.at[0],
            dst_ref=peaks.at[d],
            send_sem=tile_send.at[d - 1],
            recv_sem=tile_recv.at[d - 1],
            device_id=tile_peer(d),
            device_id_type=MESH,
        )
        for d in range(1, tiles)
    ]
    for copy in crossed:
        copy.start()
    for copy in scattered + gathered + spread:
        copy.wait_send()

    def finish(k, carry):
        for stage in range(bits):
            for copy in copies(k, stage):
                copy.wait_send()
        return carry

    lax.fori_loop(0, turns, finish, 0)
    for d in range(1, groups):
        square_copy(d).wait_send()
    for d in range(1, tiles):
        crossed[d - 1].wait()
        top = jnp.maximum(top, peaks[d])
    peak_ref[...] = top.T[: turns - 1]


def shards(traits, covariates, genotypes, shuffles):
    groups, tiles = lax.axis_size("samp"), lax.axis_size("tile")
    bits = groups.bit_length() - 1
    turns = shuffles.shape[0] + 1
    local, n_traits = traits.shape
    width = genotypes.shape[1]
    used = covariates.shape[1] + 1
    own = n_traits // groups
    areas = parts_of(bits, own, width)
    bufs = []
    for _, part_rows, part_lanes in areas:
        size = (part_rows.stop - part_rows.start, part_lanes.stop - part_lanes.start)
        for stage in range(bits):
            lot = 2 ** (bits - 1 - stage)
            bufs.append(pltpu.VMEM((turns, 2, lot) + size, F32))
            bufs.append(pltpu.VMEM((turns, lot) + size, F32))
    n_blocks = (n_traits // tiles + width) // LANES + 1
    slots = n_blocks * (used // 8) + -(-n_blocks * (used % 8) // 8)
    quota = -(-slots // groups)
    vmem = pl.BlockSpec(memory_space=pltpu.VMEM)
    sems = pltpu.SemaphoreType.DMA((turns, len(areas), bits))
    flat = pltpu.SemaphoreType.DMA((groups - 1,))
    pair = pltpu.SemaphoreType.DMA((max(2 * (tiles - 1), 1),))
    return pl.pallas_call(
        functools.partial(scan_kernel, groups, tiles, local * groups, used, areas),
        out_shape=(
            jax.ShapeDtypeStruct((own, width), F32),
            jax.ShapeDtypeStruct((turns - 1, own), F32),
        ),
        in_specs=[pl.BlockSpec(memory_space=pl.ANY)] * 4,
        out_specs=(vmem, vmem),
        scratch_shapes=[
            pltpu.VMEM((local, n_traits), BF16),
            pltpu.VMEM((used - 1, local), BF16),
            pltpu.VMEM((local, width), jnp.int32),
            pltpu.VMEM((turns - 1, local), jnp.int32),
            pltpu.SemaphoreType.DMA((4,)),
            pltpu.VMEM((local, LANES), BF16),
            pltpu.VMEM((quota * groups, 8, LANES), F32),
            pltpu.VMEM((groups - 1, quota, 8, LANES), F32),
            pltpu.VMEM((quota, 8, LANES), F32),
            pltpu.VMEM((tiles, quota * groups, 8, LANES), F32),
            pltpu.VMEM((LANES, n_traits + width), F32),
            pltpu.VMEM((LANES, n_traits + width), BF16),
            pltpu.VMEM((n_traits, local), BF16),
            pltpu.VMEM((local, width), BF16),
            pltpu.VMEM((local, width), BF16),
            pltpu.VMEM((turns, own, width), F32),
            pltpu.VMEM((own, width), F32),
            pltpu.VMEM((LANES // 2, LANES), F32),
            pltpu.VMEM((groups, 8, LANES), F32),
            pltpu.VMEM((groups, 8, LANES), F32),
            pltpu.VMEM((LANES, LANES), F32),
            pltpu.VMEM((tiles, own, LANES), F32),
            pltpu.SemaphoreType.DMA((4, groups - 1)),
            flat,
            flat,
            pair,
            pair,
            sems,
            sems,
            *bufs,
        ],
        compiler_params=pltpu.CompilerParams(
            collective_id=0, has_side_effects=True, vmem_limit_bytes=60 * 1024 * 1024
        ),
        name="scan",
    )(traits, covariates.T, genotypes, shuffles)


def solution(mesh):
    placed = (P("samp", None), P("samp", None), P("samp", "tile"), P(None, "samp"))
    return jax.shard_map(
        shards,
        mesh=mesh,
        in_specs=placed,
        out_specs=(P("samp", "tile"), P(None, "samp")),
        check_vma=False,
    )
```

time: 101 us -> 86.7 us (0.86)
  Pallas kernels: 95.6 us -> 83.1 us
  local copies, waits for them, and re-layouts: 4.42 us -> 2.74 us
    pallas_call x1, Pallas kernels: 95.6 us -> 83.1 us  [shards(): pl.pallas_call(functools.partial(scan_kernel, groups, tiles, local * grou...]
    unnamed x3 -> x2, local copies, waits for them, and re-layouts: 4.42 us -> 2.74 us
where the time goes in v1:
time: 86.7 us; the launch traced here: 86.5 us
  Pallas kernels  83.1 us (96%)
  local copies, waits for them, and re-layouts  2.74 us (3%)
    pallas_call x1, Pallas kernels, shards(): pl.pallas_call(functools.partial(scan_kernel, groups, tiles, local * grou...  83.1 us
    unnamed x2, local copies, waits for them, and re-layouts  2.74 us

profile of v1, /device:TPU:0, one launch (start us, length us, event | category | flops | bytes accessed | tf_op | source)
XLA Modules:
  0.0 86.5 jit_solution(9214136138436036341)
XLA Ops:
  0.6 83.1 %scan.1 = (f32[64,256]{1,0:T(8,128)}, f32[6,64]{1,0:T(8,128)}) custom-call(bf16[1024,1024]{1,0:T(8,128)(2,1)} %t_hbm.1, bf16[32,1024]{1,0:T(8,128)(2,1)} %bitcast.1, s32[1024,256]{1,0:T(8,128)} %g_hbm.1, s32[6,1024]{1,0:T(8,128)} %order_hbm.1), custom_call_target="tpu_custom_call" | custom-call | tf_op jit(solution)/shard_map/scan/pallas_call | solution.py:425
  83.8 1.5 %copy.8 = f32[64,256]{1,0:T(8,128)} copy(f32[64,256]{1,0:T(8,128)} %get-tuple-element.4) | data formatting | bytes 131072
  85.2 1.3 %copy.9 = f32[6,64]{1,0:T(8,128)} copy(f32[6,64]{1,0:T(8,128)} %get-tuple-element.5) | data formatting | bytes 3072

commit v2 on v1

--- a/solution.py
+++ b/solution.py
@@ -18,9 +18,12 @@
 def parts_of(bits, own, width):
     cut, half = own - max(8, own // 32 * 8), width // 2
     low, high, rest = tuple(range(2)), tuple(range(2, bits)), tuple(range(3, bits))
+    mid = cut // 16 * 8
     return (
-        ((0, 1) + high, slice(0, cut), slice(0, half)),
-        ((1, 0) + high, slice(0, cut), slice(half, width)),
+        ((0, 1) + high, slice(0, mid), slice(0, half)),
+        ((1, 0) + high, slice(0, mid), slice(half, width)),
+        ((0, 1) + high, slice(mid, cut), slice(0, half)),
+        ((1, 0) + high, slice(mid, cut), slice(half, width)),
         (high + low, slice(cut, own), slice(0, half)),
         ((2, 1, 0) + rest, slice(cut, own), slice(half, width)),
     )
@@ -115,34 +118,29 @@
         bit = areas[p][0][stage]
         return lax.rem(me // 2**bit, 2), 2**bit
 
-    def copies(k, stage):
-        out = []
+    def copy_of(k, p, stage):
+        b, far = side(p, stage)
+        return pltpu.make_async_remote_copy(
+            src_ref=source(p, stage).at[k, 1 - b],
+            dst_ref=target(p, stage).at[k],
+            send_sem=send.at[k, p, stage],
+            recv_sem=recv.at[k, p, stage],
+            device_id={"samp": me + (1 - 2 * b) * far},
+            device_id_type=MESH,
+        )
+
+    def begin(k):
         for p in range(n_parts):
-            b, far = side(p, stage)
-            out.append(
-                pltpu.make_async_remote_copy(
-                    src_ref=source(p, stage).at[k, 1 - b],
-                    dst_ref=target(p, stage).at[k],
-                    send_sem=send.at[k, p, stage],
-                    recv_sem=recv.at[k, p, stage],
-                    device_id={"samp": me + (1 - 2 * b) * far},
-                    device_id_type=MESH,
-                )
-            )
-        return out
-
-    def begin(k, stage):
-        for copy in copies(k, stage):
-            copy.start()
-
-    def collect(k, stage):
-        for copy in copies(k, stage):
-            copy.wait_recv()
+            copy_of(k, p, 0).start()
+
+    def advance(k, stage):
         for p in range(n_parts):
+            copy_of(k, p, stage).wait_recv()
             b, _ = side(p, stage)
             total = source(p, stage)[k, b] + target(p, stage)[k]
             if stage < bits - 1:
                 source(p, stage + 1)[k] = total.reshape(source(p, stage + 1).shape[1:])
+                copy_of(k, p, stage + 1).start()
             else:
                 found[k, areas[p][1], areas[p][2]] = total[0]
 
@@ -161,6 +159,15 @@
                         part_rows, part_lanes
                     ]
 
+    def permute(k, rows):
+        order = order_ref[pl.ds(k - 1, 1), :] - me * local
+        for i in range(local // step):
+            row = lax.broadcasted_iota(jnp.int32, (step, local), 0) + i * step
+            hot = jnp.where(row == order, 1.0, 0.0).astype(BF16)
+            moved[i * step : (i + 1) * step, : rows.shape[1]] = jnp.dot(
+                hot, rows, preferred_element_type=F32
+            ).astype(BF16)
+
     step = min(256, local)
     for i in range(local // step):
         at = slice(i * step, (i + 1) * step)
@@ -184,7 +191,8 @@
     ]
     for copy in scattered:
         copy.start()
-    begin(0, 0)
+    begin(0)
+    permute(1, jnp.concatenate([dose.astype(BF16), design[...]], axis=1))
     total = parts[pl.ds(me * quota, quota)]
     for d in range(1, groups):
         scattered[d - 1].wait_recv()
@@ -200,8 +208,7 @@
     rhs[...] = jnp.zeros(rhs.shape, F32)
     gram_ref[...] = jnp.zeros(gram_ref.shape, F32)
     coef[...] = jnp.zeros(coef.shape, BF16)
-    collect(0, 0)
-    begin(0, 1)
+    advance(0, 0)
     for copy in gathered:
         copy.wait_recv()
 
@@ -218,8 +225,6 @@
     spread = [spread_copy(d) for d in range(1, tiles)]
     for copy in spread:
         copy.start()
-    collect(0, 1)
-    begin(0, 2)
 
     half = LANES // 2
     last = n_blocks - 1
@@ -252,21 +257,28 @@
     coef[: 8 * strips, :] = jnp.dot(
         inverse, rhs[...], precision=HIGHEST, preferred_element_type=F32
     ).astype(BF16)
-    collect(0, 2)
-    begin(0, 3)
-
+
+    advance(0, 1)
     sq_t = jnp.zeros((1, traits), F32)
+    for i in range(local // step):
+        at = slice(i * step, (i + 1) * step)
+        resid = t_ref[at, :].astype(F32) - jnp.dot(
+            design[at, :], coef[:, :traits], preferred_element_type=F32
+        )
+        sq_t = sq_t + jnp.sum(resid * resid, axis=0, keepdims=True)
+        rt[:, at] = resid.astype(BF16).T
+    resid = moved[:, :width].astype(F32) - jnp.dot(
+        moved[:, width:], coef[:, traits:], preferred_element_type=F32
+    )
+    cross(1, resid.astype(BF16))
+    begin(1)
+    advance(0, 2)
     sq_g = jnp.zeros((1, width), F32)
     for i in range(local // step):
         at = slice(i * step, (i + 1) * step)
-        d = design[at, :]
-        resid = t_ref[at, :].astype(F32) - jnp.dot(
-            d, coef[:, :traits], preferred_element_type=F32
-        )
-        sq_t = sq_t + jnp.sum(resid * resid, axis=0, keepdims=True)
-        rt[:, at] = resid.astype(BF16).T
-        dose = g_ref[at, :].astype(F32)
-        resid = dose - jnp.dot(d, coef[:, traits:], preferred_element_type=F32)
+        resid = g_ref[at, :].astype(F32) - jnp.dot(
+            design[at, :], coef[:, traits:], preferred_element_type=F32
+        )
         sq_g = sq_g + jnp.sum(resid * resid, axis=0, keepdims=True)
         rg[at, :] = resid.astype(BF16)
 
@@ -291,15 +303,8 @@
 
     note_squares()
     squares[0] = notes[me]
-
-    def permute(k):
-        order = order_ref[pl.ds(k - 1, 1), :] - me * local
-        for i in range(local // step):
-            row = lax.broadcasted_iota(jnp.int32, (step, local), 0) + i * step
-            hot = jnp.where(row == order, 1.0, 0.0).astype(BF16)
-            moved[i * step : (i + 1) * step, :] = jnp.dot(
-                hot, rg[...], preferred_element_type=F32
-            ).astype(BF16)
+    for d in range(1, groups):
+        square_copy(d).start()
 
     lead = pl.multiple_of(me * own // LANES * LANES, LANES)
     shift = pl.multiple_of(lax.rem(me * own, LANES), 8)
@@ -325,31 +330,25 @@
             preferred_element_type=F32,
         )
 
+    correct()
+
     def turn(t, carry):
         @pl.when(t < turns)
         def _():
-            permute(t)
-            cross(t, moved[...])
-            begin(t, 0)
-
-        @pl.when(t == 1)
-        def _():
-            for d in range(1, groups):
-                square_copy(d).start()
-            correct()
+            permute(t, rg[...])
+            cross(t, moved[:, :width])
+            begin(t)
 
         for stage in range(bits):
             k = t - 1 - stage
 
             @pl.when(jnp.logical_and(k >= (0 if stage > 2 else 1), k < turns))
             def _():
-                collect(k, stage)
-                if stage < bits - 1:
-                    begin(k, stage + 1)
+                advance(k, stage)
 
         return carry
 
-    lax.fori_loop(1, turns + bits, turn, 0)
+    lax.fori_loop(2, turns + bits, turn, 0)
 
     total = squares[0]
     for d in range(1, groups):
@@ -385,9 +384,9 @@
         copy.wait_send()
 
     def finish(k, carry):
-        for stage in range(bits):
-            for copy in copies(k, stage):
-                copy.wait_send()
+        for p in range(n_parts):
+            for stage in range(bits):
+                copy_of(k, p, stage).wait_send()
         return carry
 
     lax.fori_loop(0, turns, finish, 0)
@@ -425,8 +424,8 @@
     return pl.pallas_call(
         functools.partial(scan_kernel, groups, tiles, local * groups, used, areas),
         out_shape=(
-            jax.ShapeDtypeStruct((own, width), F32),
-            jax.ShapeDtypeStruct((turns - 1, own), F32),
+            pltpu.VMEM((own, width), F32),
+            pltpu.VMEM((turns - 1, own), F32),
         ),
         in_specs=[pl.BlockSpec(memory_space=pl.ANY)] * 4,
         out_specs=(vmem, vmem),
@@ -445,7 +444,7 @@
             pltpu.VMEM((LANES, n_traits + width), BF16),
             pltpu.VMEM((n_traits, local), BF16),
             pltpu.VMEM((local, width), BF16),
-            pltpu.VMEM((local, width), BF16),
+            pltpu.VMEM((local, width + LANES), BF16),
             pltpu.VMEM((turns, own, width), F32),
             pltpu.VMEM((own, width), F32),
             pltpu.VMEM((LANES // 2, LANES), F32),

time: 86.7 us -> 81.2 us (0.937)
  Pallas kernels: 83.1 us -> 79.2 us
  local copies, waits for them, and re-layouts: 2.74 us -> 1.22 us
    pallas_call x1, Pallas kernels: 83.1 us -> 79.2 us  [shards(): pl.pallas_call(functools.partial(scan_kernel, groups, tiles, local * grou...]
    unnamed x2, local copies, waits for them, and re-layouts: 2.74 us -> 1.22 us
where the time goes in v2:
time: 81.2 us; the launch traced here: 81.1 us
  Pallas kernels  79.2 us (98%)
  local copies, waits for them, and re-layouts  1.22 us (2%)
    pallas_call x1, Pallas kernels, shards(): pl.pallas_call(functools.partial(scan_kernel, groups, tiles, local * grou...  79.2 us

profile of v2, /device:TPU:0, one launch (start us, length us, event | category | flops | bytes accessed | tf_op | source)
XLA Modules:
  0.0 81.1 jit_solution(10583549985398189187)
XLA Ops:
  0.6 79.2 %scan.1 = (f32[64,256]{1,0:T(8,128)S(1)}, f32[6,64]{1,0:T(8,128)S(1)}) custom-call(bf16[1024,1024]{1,0:T(8,128)(2,1)} %t_hbm.1, bf16[32,1024]{1,0:T(8,128)(2,1)} %bitcast.1, s32[1024,256]{1,0:T(8,128)} %g_hbm.1, s32[6,1024]{1,0:T(8,128)} %order_hbm.1), custom_call_target="tpu_custom_call" | custom-call | tf_op jit(solution)/shard_map/scan/pallas_call | solution.py:424
  79.9 0.6 copy.8
  80.5 0.6 copy.9

commit v3 on v2

--- a/solution.py
+++ b/solution.py
@@ -17,36 +17,41 @@
 
 def parts_of(bits, own, width):
     cut, half = own - max(8, own // 32 * 8), width // 2
-    low, high, rest = tuple(range(2)), tuple(range(2, bits)), tuple(range(3, bits))
-    mid = cut // 16 * 8
+    mid = (cut // 8 + 1) // 2 * 8
+    ones = tuple((bit,) for bit in range(bits))
+    far = ones[2:-2] + ((bits - 2, bits - 1),)
+    x_first, y_first = ones[:2] + far, ones[1::-1] + far
     return (
-        ((0, 1) + high, slice(0, mid), slice(0, half)),
-        ((1, 0) + high, slice(0, mid), slice(half, width)),
-        ((0, 1) + high, slice(mid, cut), slice(0, half)),
-        ((1, 0) + high, slice(mid, cut), slice(half, width)),
-        (high + low, slice(cut, own), slice(0, half)),
-        ((2, 1, 0) + rest, slice(cut, own), slice(half, width)),
+        (x_first, slice(0, mid), slice(0, half)),
+        (y_first, slice(0, mid), slice(half, width)),
+        (ones[2:] + ones[:2], slice(cut, own), slice(0, half)),
+        (ones[2::-1] + ones[3:], slice(cut, own), slice(half, width)),
+        (x_first, slice(mid, cut), slice(0, half)),
+        (y_first, slice(mid, cut), slice(half, width)),
     )
 
 
+HALVES = ((0, 1, 2, 3), (4, 5))
+
+
 def place_of(order, g):
-    at = [(g >> bit) & 1 for bit in order]
+    at = [g >> some[0] & 2 ** len(some) - 1 for some in order]
     rest = 0
-    for bit in at[1:]:
-        rest = 2 * rest + bit
+    for digit, some in zip(at[1:], order[1:]):
+        rest = 2 ** len(some) * rest + digit
     return at[0], rest
 
 
 def scan_kernel(
     groups, tiles, samples, used, areas, t_hbm, c_hbm, g_hbm, order_hbm, score_ref, peak_ref,
     t_ref, c_ref, g_ref, order_ref, load, design, parts, landed, mine, full, rhs, coef, rt, rg,
-    moved, found, fix, gram_ref, notes, squares, column, peaks, sum_sems, sq_send, sq_recv,
-    tile_send, tile_recv, send, recv, *bufs
+    moved, found, fix, gram_part, gram_landed, gram_sum, gram_ref, notes, squares, column, gain_g,
+    peaks, flat, tile_send, tile_recv, send, recv, *bufs
 ):
     me = lax.axis_index("samp")
     my_tile = lax.axis_index("tile")
     turns, width, n_parts = found.shape[0], found.shape[2], len(areas)
-    bits = len(areas[0][0])
+    bits = groups.bit_length() - 1
     local, traits = t_ref.shape
     own = traits // groups
     share = traits // tiles
@@ -81,7 +86,7 @@
     design[...] = design_t.T.astype(BF16)
     design_t = design_t[: -(-used // 16) * 16].astype(BF16)
     n_t, n_g = share // LANES, width // LANES
-    n_blocks = n_t + n_g + 1
+    n_blocks = n_t + n_g
     whole, rest = used // 8, used % 8
     strips = -(-used // 8)
 
@@ -96,7 +101,6 @@
     for block in (
         t_ref[:, pl.ds(pl.multiple_of(my_tile * share, LANES), share)],
         dose.astype(BF16),
-        design[...],
     ):
         block = jnp.dot(design_t, block, preferred_element_type=F32)
         for c in range(block.shape[1] // LANES):
@@ -108,39 +112,72 @@
                 parts[slot, row : row + 1, :] = block[8 * whole + r : 8 * whole + r + 1, at]
         first += block.shape[1] // LANES
 
+    gram = jnp.dot(design_t, design[...], preferred_element_type=F32)
+    gram_part[...] = jnp.zeros(gram_part.shape, F32)
+    lots = gram_part.shape[1]
+    pack = LANES // (8 * strips)
+    for r in range(strips):
+        at = slice(r % pack * 8 * strips, (r % pack + 1) * 8 * strips)
+        gram_part[r // pack // lots, r // pack % lots, :, at] = gram[
+            8 * r : 8 * r + 8, : 8 * strips
+        ]
+
+    def await_all(sem, like):
+        pltpu.make_async_copy(like, like, flat.at[sem]).wait()
+
+    starts = [sum(2 * len(area[0]) for area in areas[:p]) for p in range(n_parts)]
+
     def source(p, stage):
-        return bufs[2 * p * bits + 2 * stage]
+        return bufs[starts[p] + 2 * stage]
 
     def target(p, stage):
-        return bufs[2 * p * bits + 2 * stage + 1]
-
-    def side(p, stage):
-        bit = areas[p][0][stage]
-        return lax.rem(me // 2**bit, 2), 2**bit
-
-    def copy_of(k, p, stage):
-        b, far = side(p, stage)
-        return pltpu.make_async_remote_copy(
-            src_ref=source(p, stage).at[k, 1 - b],
-            dst_ref=target(p, stage).at[k],
-            send_sem=send.at[k, p, stage],
-            recv_sem=recv.at[k, p, stage],
-            device_id={"samp": me + (1 - 2 * b) * far},
-            device_id_type=MESH,
-        )
-
-    def begin(k):
-        for p in range(n_parts):
-            copy_of(k, p, 0).start()
-
-    def advance(k, stage):
-        for p in range(n_parts):
-            copy_of(k, p, stage).wait_recv()
-            b, _ = side(p, stage)
-            total = source(p, stage)[k, b] + target(p, stage)[k]
-            if stage < bits - 1:
+        return bufs[starts[p] + 2 * stage + 1]
+
+    def digit(p, stage):
+        some = areas[p][0][stage]
+        return lax.rem(me // 2 ** some[0], 2 ** len(some)), 2 ** len(some), 2 ** some[0]
+
+    def copies(k, p, stage):
+        mine, n, far = digit(p, stage)
+        first = sum(2 ** len(some) - 1 for some in areas[p][0][:stage])
+        out = []
+        for d in range(1, n):
+            other = lax.rem(mine + d, n)
+            at = lax.rem(k, 2), p, first + d - 1
+            out.append(
+                pltpu.make_async_remote_copy(
+                    src_ref=source(p, stage).at[k, other],
+                    dst_ref=target(p, stage).at[k, d - 1],
+                    send_sem=send.at[at],
+                    recv_sem=recv.at[at],
+                    device_id={"samp": me + (other - mine) * far},
+                    device_id_type=MESH,
+                )
+            )
+        return out
+
+    def begin(k, part):
+        for p in HALVES[part]:
+            for copy in copies(k, p, 0):
+                copy.start()
+
+    def advance(k, part, stage, first=False):
+        for p in HALVES[part]:
+            if stage >= len(areas[p][0]):
+                continue
+            for copy in copies(k, p, stage):
+                copy.wait_recv()
+            if not first:
+                for copy in copies(k - 1, p, stage):
+                    copy.wait_send()
+            mine, n, _ = digit(p, stage)
+            total = source(p, stage)[k, mine]
+            for d in range(1, n):
+                total = total + target(p, stage)[k, d - 1]
+            if stage < len(areas[p][0]) - 1:
                 source(p, stage + 1)[k] = total.reshape(source(p, stage + 1).shape[1:])
-                copy_of(k, p, stage + 1).start()
+                for copy in copies(k, p, stage + 1):
+                    copy.start()
             else:
                 found[k, areas[p][1], areas[p][2]] = total[0]
 
@@ -159,6 +196,39 @@
                         part_rows, part_lanes
                     ]
 
+    pl.semaphore_wait(barrier, groups + tiles - 2)
+
+    odd = lax.rem(my_tile, 2)
+
+    def gram_copy(d):
+        return pltpu.make_async_remote_copy(
+            src_ref=gram_part.at[odd],
+            dst_ref=gram_landed.at[d - 1],
+            send_sem=flat.at[4],
+            recv_sem=flat.at[5],
+            device_id=samp_peer(d),
+            device_id_type=MESH,
+        )
+
+    for d in range(1, groups):
+        gram_copy(d).start()
+
+    def sum_copy(d, source, target, stage):
+        return pltpu.make_async_remote_copy(
+            src_ref=source,
+            dst_ref=target,
+            send_sem=flat.at[2 * stage],
+            recv_sem=flat.at[2 * stage + 1],
+            device_id=samp_peer(d),
+            device_id_type=MESH,
+        )
+
+    scattered = [
+        sum_copy(d, parts.at[pl.ds(lax.rem(me + d, groups) * quota, quota)], landed.at[d - 1], 0)
+        for d in range(1, groups)
+    ]
+    for copy in scattered:
+        copy.start()
     def permute(k, rows):
         order = order_ref[pl.ds(k - 1, 1), :] - me * local
         for i in range(local // step):
@@ -173,29 +243,12 @@
         at = slice(i * step, (i + 1) * step)
         rt[:, at] = t_ref[at, :].T
     cross(0, (dose - 1.0).astype(BF16))
-    pl.semaphore_wait(barrier, groups + tiles - 2)
-
-    def sum_copy(d, source, target, stage):
-        return pltpu.make_async_remote_copy(
-            src_ref=source,
-            dst_ref=target,
-            send_sem=sum_sems.at[2 * stage, d - 1],
-            recv_sem=sum_sems.at[2 * stage + 1, d - 1],
-            device_id=samp_peer(d),
-            device_id_type=MESH,
-        )
-
-    scattered = [
-        sum_copy(d, parts.at[pl.ds(lax.rem(me + d, groups) * quota, quota)], landed.at[d - 1], 0)
-        for d in range(1, groups)
-    ]
-    for copy in scattered:
-        copy.start()
-    begin(0)
+    begin(0, 0)
+    begin(0, 1)
     permute(1, jnp.concatenate([dose.astype(BF16), design[...]], axis=1))
     total = parts[pl.ds(me * quota, quota)]
+    await_all(1, landed)
     for d in range(1, groups):
-        scattered[d - 1].wait_recv()
         total = total + landed[d - 1]
     mine[...] = total
     full[my_tile, pl.ds(me * quota, quota)] = total
@@ -205,12 +258,41 @@
     ]
     for copy in gathered:
         copy.start()
+    await_all(5, gram_landed)
+    total = gram_part[odd]
+    for d in range(1, groups):
+        total = total + gram_landed[d - 1]
+    gram_sum[odd] = total
+    swap = pltpu.make_async_remote_copy(
+        src_ref=gram_sum.at[odd],
+        dst_ref=gram_sum.at[odd],
+        send_sem=tile_send.at[2 * (tiles - 1)],
+        recv_sem=tile_recv.at[2 * (tiles - 1)],
+        device_id={"tile": my_tile + 1 - 2 * odd},
+        device_id_type=MESH,
+    )
+    swap.start()
     rhs[...] = jnp.zeros(rhs.shape, F32)
     gram_ref[...] = jnp.zeros(gram_ref.shape, F32)
     coef[...] = jnp.zeros(coef.shape, BF16)
-    advance(0, 0)
-    for copy in gathered:
-        copy.wait_recv()
+    half = LANES // 2
+    swap.wait_recv()
+    for r in range(strips):
+        at = slice(r % pack * 8 * strips, (r % pack + 1) * 8 * strips)
+        gram_ref[8 * r : 8 * r + 8, : 8 * strips] = gram_sum[r // pack // lots, r // pack % lots][
+            :, at
+        ]
+    gram = gram_ref[: 8 * strips, :]
+    sub = lax.broadcasted_iota(jnp.int32, gram.shape, 0)
+    lane = lax.broadcasted_iota(jnp.int32, gram.shape, 1)
+    gram = jnp.where(lane == sub + half, 1.0, gram)
+    for j in range(used):
+        row = gram[j : j + 1, :] * (1.0 / gram[j : j + 1, j : j + 1])
+        gram = jnp.where(sub == j, row, gram - gram[:, j : j + 1] * row)
+    inverse = jnp.where(lane >= half, gram, 0.0)
+    advance(0, 0, 0, True)
+    advance(0, 1, 0, True)
+    await_all(3, landed)
 
     def spread_copy(d):
         return pltpu.make_async_remote_copy(
@@ -226,21 +308,6 @@
     for copy in spread:
         copy.start()
 
-    half = LANES // 2
-    last = n_blocks - 1
-    for r in range(whole):
-        gram_ref[8 * r : 8 * r + 8, :] = full[my_tile, last * whole + r]
-    for r in range(rest):
-        slot, row = spot(last, r)
-        gram_ref[8 * whole + r : 8 * whole + r + 1, :] = full[my_tile, slot, row : row + 1, :]
-    gram = gram_ref[: 8 * strips, :]
-    sub = lax.broadcasted_iota(jnp.int32, gram.shape, 0)
-    lane = lax.broadcasted_iota(jnp.int32, gram.shape, 1)
-    gram = jnp.where(lane == sub + half, 1.0, gram)
-    for j in range(used):
-        row = gram[j : j + 1, :] * (1.0 / gram[j : j + 1, j : j + 1])
-        gram = jnp.where(sub == j, row, gram - gram[:, j : j + 1] * row)
-    inverse = jnp.where(lane >= half, gram, 0.0)
     for copy in spread:
         copy.wait_recv()
     for tile in range(tiles + 1):
@@ -258,7 +325,8 @@
         inverse, rhs[...], precision=HIGHEST, preferred_element_type=F32
     ).astype(BF16)
 
-    advance(0, 1)
+    advance(0, 0, 1, True)
+    advance(0, 1, 1, True)
     sq_t = jnp.zeros((1, traits), F32)
     for i in range(local // step):
         at = slice(i * step, (i + 1) * step)
@@ -271,8 +339,10 @@
         moved[:, width:], coef[:, traits:], preferred_element_type=F32
     )
     cross(1, resid.astype(BF16))
-    begin(1)
-    advance(0, 2)
+    begin(1, 0)
+    begin(1, 1)
+    advance(0, 0, 2, True)
+    advance(0, 1, 2, True)
     sq_g = jnp.zeros((1, width), F32)
     for i in range(local // step):
         at = slice(i * step, (i + 1) * step)
@@ -295,8 +365,8 @@
         return pltpu.make_async_remote_copy(
             src_ref=notes.at[lax.rem(me + d, groups)],
             dst_ref=squares.at[d],
-            send_sem=sq_send.at[d - 1],
-            recv_sem=sq_recv.at[d - 1],
+            send_sem=flat.at[6],
+            recv_sem=flat.at[7],
             device_id=samp_peer(d),
             device_id_type=MESH,
         )
@@ -332,41 +402,80 @@
 
     correct()
 
+    peaks[0] = jnp.zeros(peaks.shape[1:], F32)
+
+    def scale():
+        total = squares[0]
+        await_all(7, squares.at[pl.ds(1, groups - 1)])
+        for d in range(1, groups):
+            total = total + squares[d]
+        gain = lax.rsqrt(total / samples + epsilon)
+        factor = math.sqrt(samples - used - 1) / samples
+        for c in range(n_g):
+            gain_g[:, c * LANES : (c + 1) * LANES] = jnp.broadcast_to(
+                gain[1 + c : 2 + c, :], (8, LANES)
+            )
+        column[...] = jnp.broadcast_to(gain.T[:, :1] * factor, column.shape)
+
+    def peak_of(k):
+        gain_t = column[pl.ds(shift, own), :]
+        peak = jnp.max(jnp.abs(found[k] * gain_g[:1, :]), axis=1, keepdims=True) * gain_t
+        pos = lax.broadcasted_iota(jnp.int32, peak.shape, 1)
+        peaks[0] = jnp.where(pos == k - 1, peak, peaks[0])
+
     def turn(t, carry):
-        @pl.when(t < turns)
+        for stage in range(3, bits):
+
+            @pl.when(t == stage - 1)
+            def _():
+                advance(0, 0, stage, True)
+                advance(0, 1, stage, True)
+
+        fresh = jnp.logical_and(t > 1, t < turns)
+
+        @pl.when(fresh)
         def _():
-            permute(t, rg[...])
-            cross(t, moved[:, :width])
-            begin(t)
-
-        for stage in range(bits):
-            k = t - 1 - stage
-
-            @pl.when(jnp.logical_and(k >= (0 if stage > 2 else 1), k < turns))
-            def _():
-                advance(k, stage)
+            begin(t, 0)
+
+        @pl.when(t + 1 < turns)
+        def _():
+            permute(t + 1, rg[...])
+            cross(t + 1, moved[:, :width])
+
+        for part in range(2):
+            if part == 1:
+
+                @pl.when(fresh)
+                def _():
+                    begin(t, 1)
+
+            for stage in range(bits):
+                back = part - 1 - stage
+                k = t + back // 2
+
+                @pl.when(jnp.logical_and(k > 0, k < turns))
+                def _():
+                    advance(k, back % 2, stage)
+
+        @pl.when(t == 2)
+        def _():
+            scale()
+
+        k = t - (bits + 1) // 2
+
+        @pl.when(k == 0)
+        def _():
+            score_ref[...] = (
+                (found[0] - fix[...]) * gain_g[:1, :] * column[pl.ds(shift, own), :][:, :1]
+            )
+
+        @pl.when(k > 0)
+        def _():
+            peak_of(k)
 
         return carry
 
-    lax.fori_loop(2, turns + bits, turn, 0)
-
-    total = squares[0]
-    for d in range(1, groups):
-        square_copy(d).wait_recv()
-        total = total + squares[d]
-    gain = lax.rsqrt(total / samples + epsilon)
-    factor = math.sqrt(samples - used - 1) / samples
-    gain_g = jnp.concatenate([gain[1 + c : 2 + c, :] for c in range(n_g)], axis=1)
-    column[...] = jnp.broadcast_to(gain.T[:, :1] * factor, column.shape)
-    gain_t = column[pl.ds(shift, own), :]
-    gain_t = gain_t[:, :1]
-    score_ref[...] = (found[0] - fix[...]) * gain_g * gain_t
-    top = jnp.zeros((own, LANES), F32)
-    pos = lax.broadcasted_iota(jnp.int32, top.shape, 1)
-    for k in range(1, turns):
-        peak = jnp.max(jnp.abs(found[k] * gain_g), axis=1, keepdims=True) * gain_t
-        top = jnp.where(pos == k - 1, peak, top)
-    peaks[0] = top
+    lax.fori_loop(1, turns + (bits + 1) // 2, turn, 0)
     crossed = [
         pltpu.make_async_remote_copy(
             src_ref=peaks.at[0],
@@ -380,18 +489,17 @@
     ]
     for copy in crossed:
         copy.start()
-    for copy in scattered + gathered + spread:
+    for copy in spread + [swap]:
         copy.wait_send()
-
-    def finish(k, carry):
-        for p in range(n_parts):
-            for stage in range(bits):
-                copy_of(k, p, stage).wait_send()
-        return carry
-
-    lax.fori_loop(0, turns, finish, 0)
-    for d in range(1, groups):
-        square_copy(d).wait_send()
+    await_all(0, landed)
+    await_all(2, landed)
+    await_all(4, gram_landed)
+    await_all(6, squares.at[pl.ds(1, groups - 1)])
+    for p in range(n_parts):
+        for stage in range(len(areas[p][0])):
+            for copy in copies(turns - 1, p, stage):
+                copy.wait_send()
+    top = peaks[0]
     for d in range(1, tiles):
         crossed[d - 1].wait()
         top = jnp.maximum(top, peaks[d])
@@ -408,19 +516,22 @@
     own = n_traits // groups
     areas = parts_of(bits, own, width)
     bufs = []
-    for _, part_rows, part_lanes in areas:
+    for order, part_rows, part_lanes in areas:
         size = (part_rows.stop - part_rows.start, part_lanes.stop - part_lanes.start)
-        for stage in range(bits):
-            lot = 2 ** (bits - 1 - stage)
-            bufs.append(pltpu.VMEM((turns, 2, lot) + size, F32))
-            bufs.append(pltpu.VMEM((turns, lot) + size, F32))
-    n_blocks = (n_traits // tiles + width) // LANES + 1
+        lot = groups
+        for some in order:
+            n = 2 ** len(some)
+            lot //= n
+            bufs.append(pltpu.VMEM((turns, n, lot) + size, F32))
+            bufs.append(pltpu.VMEM((turns, n - 1, lot) + size, F32))
+    n_blocks = (n_traits // tiles + width) // LANES
+    strips = -(-used // 8)
+    lots = -(-strips // (LANES // (8 * strips) * 2))
     slots = n_blocks * (used // 8) + -(-n_blocks * (used % 8) // 8)
     quota = -(-slots // groups)
     vmem = pl.BlockSpec(memory_space=pltpu.VMEM)
-    sems = pltpu.SemaphoreType.DMA((turns, len(areas), bits))
-    flat = pltpu.SemaphoreType.DMA((groups - 1,))
-    pair = pltpu.SemaphoreType.DMA((max(2 * (tiles - 1), 1),))
+    sems = pltpu.SemaphoreType.DMA((2, len(areas), bits + 1))
+    pair = pltpu.SemaphoreType.DMA((2 * tiles - 1,))
     return pl.pallas_call(
         functools.partial(scan_kernel, groups, tiles, local * groups, used, areas),
         out_shape=(
@@ -447,14 +558,16 @@
             pltpu.VMEM((local, width + LANES), BF16),
             pltpu.VMEM((turns, own, width), F32),
             pltpu.VMEM((own, width), F32),
+            pltpu.VMEM((2, lots, 8, LANES), F32),
+            pltpu.VMEM((groups - 1, lots, 8, LANES), F32),
+            pltpu.VMEM((2, lots, 8, LANES), F32),
             pltpu.VMEM((LANES // 2, LANES), F32),
             pltpu.VMEM((groups, 8, LANES), F32),
             pltpu.VMEM((groups, 8, LANES), F32),
             pltpu.VMEM((LANES, LANES), F32),
+            pltpu.VMEM((8, width), F32),
             pltpu.VMEM((tiles, own, LANES), F32),
-            pltpu.SemaphoreType.DMA((4, groups - 1)),
-            flat,
-            flat,
+            pltpu.SemaphoreType.DMA((8,)),
             pair,
             pair,
             sems,

time: 81.2 us -> 80.1 us (0.986)
  Pallas kernels: 79.2 us -> 78.1 us
    pallas_call x1, Pallas kernels: 79.2 us -> 78.1 us  [shards(): pl.pallas_call(functools.partial(scan_kernel, groups, tiles, local * grou...]
where the time goes in v3:
time: 80.1 us; the launch traced here: 80 us
  Pallas kernels  78.1 us (98%)
  local copies, waits for them, and re-layouts  1.22 us (2%)
    pallas_call x1, Pallas kernels, shards(): pl.pallas_call(functools.partial(scan_kernel, groups, tiles, local * grou...  78.1 us

profile of v3, /device:TPU:0, one launch (start us, length us, event | category | flops | bytes accessed | tf_op | source)
XLA Modules:
  0.0 80.0 jit_solution(1957399728966540432)
XLA Ops:
  0.6 78.1 %scan.1 = (f32[64,256]{1,0:T(8,128)S(1)}, f32[6,64]{1,0:T(8,128)S(1)}) custom-call(bf16[1024,1024]{1,0:T(8,128)(2,1)} %t_hbm.1, bf16[32,1024]{1,0:T(8,128)(2,1)} %bitcast.1, s32[1024,256]{1,0:T(8,128)} %g_hbm.1, s32[6,1024]{1,0:T(8,128)} %order_hbm.1), custom_call_target="tpu_custom_call" | custom-call | tf_op jit(solution)/shard_map/scan/pallas_call | solution.py:535
  78.8 0.6 copy.8
  79.4 0.6 copy.9

commit v4 on v3

--- a/solution.py
+++ b/solution.py
@@ -44,7 +44,7 @@
 
 def scan_kernel(
     groups, tiles, samples, used, areas, t_hbm, c_hbm, g_hbm, order_hbm, score_ref, peak_ref,
-    t_ref, c_ref, g_ref, order_ref, load, design, parts, landed, mine, full, rhs, coef, rt, rg,
+    t_ref, c_ref, g_ref, order_ref, load, design, parts_t, parts_g, landed_t, landed_g, mine, full, rhs, coef, rt, rg,
     moved, found, fix, gram_part, gram_landed, gram_sum, gram_ref, notes, squares, column, gain_g,
     peaks, flat, tile_send, tile_recv, send, recv, *bufs
 ):
@@ -54,8 +54,11 @@
     bits = groups.bit_length() - 1
     local, traits = t_ref.shape
     own = traits // groups
-    share = traits // tiles
-    quota = parts.shape[0] // groups
+    pairs = tiles // 2
+    share = traits // pairs
+    quota_t, quota_g = parts_t.shape[0] // groups, parts_g.shape[0] // groups
+    odd, pair = lax.rem(my_tile, 2), my_tile // 2
+    other = my_tile + 1 - 2 * odd
 
     def samp_peer(d):
         return {"samp": lax.rem(me + d, groups)}
@@ -68,12 +71,21 @@
         pl.semaphore_signal(barrier, inc=1, device_id=samp_peer(d), device_id_type=MESH)
     for d in range(1, tiles):
         pl.semaphore_signal(barrier, inc=1, device_id=tile_peer(d), device_id_type=MESH)
-    loads = [
-        pltpu.make_async_copy(a, b, load.at[i])
-        for i, (a, b) in enumerate(
-            ((c_hbm, c_ref), (t_hbm, t_ref), (g_hbm, g_ref), (order_hbm, order_ref))
-        )
-    ]
+    for d in range(1, groups):
+        pl.semaphore_signal(
+            barrier,
+            inc=1,
+            device_id={"samp": lax.rem(me + d, groups), "tile": other},
+            device_id_type=MESH,
+        )
+    chunk = local // 4
+    pieces = [(c_hbm, c_ref)]
+    for i in range(4):
+        at = pl.ds(i * chunk, chunk)
+        pieces.append((g_hbm.at[at], g_ref.at[at]))
+        pieces.append((t_hbm.at[at], t_ref.at[at]))
+    pieces.append((order_hbm, order_ref))
+    loads = [pltpu.make_async_copy(a, b, load.at[i]) for i, (a, b) in enumerate(pieces)]
     for copy in loads:
         copy.start()
     for copy in loads:
@@ -86,41 +98,41 @@
     design[...] = design_t.T.astype(BF16)
     design_t = design_t[: -(-used // 16) * 16].astype(BF16)
     n_t, n_g = share // LANES, width // LANES
-    n_blocks = n_t + n_g
     whole, rest = used // 8, used % 8
     strips = -(-used // 8)
 
     def spot(c, r):
         at = c * rest + r
-        return n_blocks * whole + at // 8, at % 8
-
-    for i in range(n_blocks * whole, parts.shape[0]):
-        parts[i] = jnp.zeros((8, LANES), F32)
+        return n_g * whole + at // 8, at % 8
+
+    for i in range(n_g * whole, parts_g.shape[0]):
+        parts_g[i] = jnp.zeros((8, LANES), F32)
     dose = g_ref[...].astype(F32)
-    first = 0
-    for block in (
-        t_ref[:, pl.ds(pl.multiple_of(my_tile * share, LANES), share)],
-        dose.astype(BF16),
-    ):
-        block = jnp.dot(design_t, block, preferred_element_type=F32)
+
+    def put(block, parts, first):
         for c in range(block.shape[1] // LANES):
             at = slice(LANES * c, LANES * c + LANES)
             for r in range(whole):
-                parts[(first + c) * whole + r] = block[8 * r : 8 * r + 8, at]
+                parts[c * whole + r] = block[8 * r : 8 * r + 8, at]
             for r in range(rest):
                 slot, row = spot(first + c, r)
-                parts[slot, row : row + 1, :] = block[8 * whole + r : 8 * whole + r + 1, at]
-        first += block.shape[1] // LANES
+                parts_g[slot, row : row + 1, :] = block[8 * whole + r : 8 * whole + r + 1, at]
+
+    put(jnp.dot(design_t, dose.astype(BF16), preferred_element_type=F32), parts_g, n_t)
+
+    @pl.when(odd == 1)
+    def _():
+        block = t_ref[:, pl.ds(pl.multiple_of(pair * share, LANES), share)]
+        put(jnp.dot(design_t, block, preferred_element_type=F32), parts_t, 0)
+        for i in range(n_t * whole, parts_t.shape[0]):
+            parts_t[i] = jnp.zeros((8, LANES), F32)
 
     gram = jnp.dot(design_t, design[...], preferred_element_type=F32)
     gram_part[...] = jnp.zeros(gram_part.shape, F32)
-    lots = gram_part.shape[1]
     pack = LANES // (8 * strips)
     for r in range(strips):
         at = slice(r % pack * 8 * strips, (r % pack + 1) * 8 * strips)
-        gram_part[r // pack // lots, r // pack % lots, :, at] = gram[
-            8 * r : 8 * r + 8, : 8 * strips
-        ]
+        gram_part[r // pack, :, at] = gram[8 * r : 8 * r + 8, : 8 * strips]
 
     def await_all(sem, like):
         pltpu.make_async_copy(like, like, flat.at[sem]).wait()
@@ -196,39 +208,44 @@
                         part_rows, part_lanes
                     ]
 
-    pl.semaphore_wait(barrier, groups + tiles - 2)
-
-    odd = lax.rem(my_tile, 2)
-
-    def gram_copy(d):
-        return pltpu.make_async_remote_copy(
-            src_ref=gram_part.at[odd],
-            dst_ref=gram_landed.at[d - 1],
-            send_sem=flat.at[4],
-            recv_sem=flat.at[5],
-            device_id=samp_peer(d),
-            device_id_type=MESH,
-        )
-
-    for d in range(1, groups):
-        gram_copy(d).start()
-
-    def sum_copy(d, source, target, stage):
+    pl.semaphore_wait(barrier, 2 * (groups - 1) + tiles - 1)
+
+    def flat_copy(d, source, target, sem, device):
         return pltpu.make_async_remote_copy(
             src_ref=source,
             dst_ref=target,
-            send_sem=flat.at[2 * stage],
-            recv_sem=flat.at[2 * stage + 1],
-            device_id=samp_peer(d),
+            send_sem=flat.at[sem],
+            recv_sem=flat.at[sem + 1],
+            device_id=device,
             device_id_type=MESH,
         )
 
-    scattered = [
-        sum_copy(d, parts.at[pl.ds(lax.rem(me + d, groups) * quota, quota)], landed.at[d - 1], 0)
-        for d in range(1, groups)
-    ]
-    for copy in scattered:
-        copy.start()
+    def g_copy(d, side, device):
+        at = pl.ds(lax.rem(me + d, groups) * quota_g, quota_g)
+        return pltpu.make_async_remote_copy(
+            src_ref=parts_g.at[at],
+            dst_ref=landed_g.at[side, d - 1],
+            send_sem=flat.at[2],
+            recv_sem=flat.at[3 + side],
+            device_id=device,
+            device_id_type=MESH,
+        )
+
+    @pl.when(odd == 1)
+    def _():
+        for d in range(1, groups):
+            flat_copy(d, gram_part, gram_landed.at[d - 1], 7, samp_peer(d)).start()
+        for d in range(1, groups):
+            at = pl.ds(lax.rem(me + d, groups) * quota_t, quota_t)
+            flat_copy(d, parts_t.at[at], landed_t.at[d - 1], 0, samp_peer(d)).start()
+            g_copy(d, 0, samp_peer(d)).start()
+
+    @pl.when(odd == 0)
+    def _():
+        for d in range(1, groups):
+            g_copy(d, 1, {"samp": lax.rem(me + d, groups), "tile": other}).start()
+        g_copy(groups, 1, {"tile": other}).start()
+
     def permute(k, rows):
         order = order_ref[pl.ds(k - 1, 1), :] - me * local
         for i in range(local // step):
@@ -246,42 +263,54 @@
     begin(0, 0)
     begin(0, 1)
     permute(1, jnp.concatenate([dose.astype(BF16), design[...]], axis=1))
-    total = parts[pl.ds(me * quota, quota)]
-    await_all(1, landed)
-    for d in range(1, groups):
-        total = total + landed[d - 1]
-    mine[...] = total
-    full[my_tile, pl.ds(me * quota, quota)] = total
-    gathered = [
-        sum_copy(d, mine, full.at[my_tile, pl.ds(me * quota, quota)], 1)
-        for d in range(1, groups)
-    ]
-    for copy in gathered:
-        copy.start()
-    await_all(5, gram_landed)
-    total = gram_part[odd]
-    for d in range(1, groups):
-        total = total + gram_landed[d - 1]
-    gram_sum[odd] = total
     swap = pltpu.make_async_remote_copy(
-        src_ref=gram_sum.at[odd],
-        dst_ref=gram_sum.at[odd],
+        src_ref=gram_sum,
+        dst_ref=gram_sum,
         send_sem=tile_send.at[2 * (tiles - 1)],
         recv_sem=tile_recv.at[2 * (tiles - 1)],
-        device_id={"tile": my_tile + 1 - 2 * odd},
+        device_id={"tile": other},
         device_id_type=MESH,
     )
-    swap.start()
+
+    @pl.when(odd == 1)
+    def _():
+        await_all(8, gram_landed)
+        total = gram_part[...]
+        for d in range(1, groups):
+            total = total + gram_landed[d - 1]
+        gram_sum[...] = total
+        swap.start()
+        await_all(1, landed_t)
+        total = parts_t[pl.ds(me * quota_t, quota_t)]
+        for d in range(1, groups):
+            total = total + landed_t[d - 1]
+        mine[:quota_t] = total
+        await_all(3, landed_g.at[0, pl.ds(0, groups - 1)])
+        total = parts_g[pl.ds(me * quota_g, quota_g)]
+        for d in range(1, groups):
+            total = total + landed_g[0, d - 1]
+        mine[quota_t : quota_t + quota_g] = total
+        await_all(4, landed_g.at[1])
+        total = landed_g[1, 0]
+        for d in range(1, groups):
+            total = total + landed_g[1, d]
+        mine[quota_t + quota_g :] = total
+        full[pair, me] = mine[...]
+        for d in range(1, groups):
+            flat_copy(d, mine, full.at[pair, me], 5, samp_peer(d)).start()
+
     rhs[...] = jnp.zeros(rhs.shape, F32)
     gram_ref[...] = jnp.zeros(gram_ref.shape, F32)
     coef[...] = jnp.zeros(coef.shape, BF16)
     half = LANES // 2
-    swap.wait_recv()
+
+    @pl.when(odd == 0)
+    def _():
+        swap.wait_recv()
+
     for r in range(strips):
         at = slice(r % pack * 8 * strips, (r % pack + 1) * 8 * strips)
-        gram_ref[8 * r : 8 * r + 8, : 8 * strips] = gram_sum[r // pack // lots, r // pack % lots][
-            :, at
-        ]
+        gram_ref[8 * r : 8 * r + 8, : 8 * strips] = gram_sum[r // pack][:, at]
     gram = gram_ref[: 8 * strips, :]
     sub = lax.broadcasted_iota(jnp.int32, gram.shape, 0)
     lane = lax.broadcasted_iota(jnp.int32, gram.shape, 1)
@@ -292,35 +321,47 @@
     inverse = jnp.where(lane >= half, gram, 0.0)
     advance(0, 0, 0, True)
     advance(0, 1, 0, True)
-    await_all(3, landed)
-
-    def spread_copy(d):
+
+    def spread_copy(d, q):
         return pltpu.make_async_remote_copy(
-            src_ref=full.at[my_tile],
-            dst_ref=full.at[my_tile],
+            src_ref=full.at[q],
+            dst_ref=full.at[q],
             send_sem=tile_send.at[tiles - 1 + d - 1],
-            recv_sem=tile_recv.at[tiles - 1 + d - 1],
+            recv_sem=tile_recv.at[tiles - 1 + q],
             device_id=tile_peer(d),
             device_id_type=MESH,
         )
 
-    spread = [spread_copy(d) for d in range(1, tiles)]
-    for copy in spread:
-        copy.start()
-
-    for copy in spread:
-        copy.wait_recv()
-    for tile in range(tiles + 1):
-        held = full.at[tile] if tile < tiles else full.at[my_tile]
-        for c in range(n_t if tile < tiles else n_g):
-            block = c + (0 if tile < tiles else n_t)
-            at = LANES * (tile * n_t + c)
+    @pl.when(odd == 1)
+    def _():
+        await_all(6, full.at[0, pl.ds(0, groups - 1)])
+        for d in range(1, tiles):
+            spread_copy(d, pair).start()
+
+    for q in range(pairs):
+
+        @pl.when(jnp.logical_or(odd == 0, pair != q))
+        def _():
+            spread_copy(1, q).wait_recv()
+
+    for q in range(pairs + 1):
+        for c in range(n_t if q < pairs else n_g):
+            at = LANES * (q * n_t + c)
             for r in range(whole):
-                rhs[half + 8 * r : half + 8 * r + 8, at : at + LANES] = held[block * whole + r]
+                i = c * whole + r
+                if q < pairs:
+                    strip = full[q, i // quota_t, i % quota_t]
+                else:
+                    strip = full[pair, i // quota_g, quota_t + (1 - odd) * quota_g + i % quota_g]
+                rhs[half + 8 * r : half + 8 * r + 8, at : at + LANES] = strip
             for r in range(rest):
-                slot, row = spot(block, r)
+                i, row = spot(c if q < pairs else n_t + c, r)
                 to = half + 8 * whole + r
-                rhs[to : to + 1, at : at + LANES] = held[slot, row : row + 1, :]
+                if q < pairs:
+                    strip = full[q, i // quota_g, quota_t + i % quota_g]
+                else:
+                    strip = full[pair, i // quota_g, quota_t + (1 - odd) * quota_g + i % quota_g]
+                rhs[to : to + 1, at : at + LANES] = strip[row : row + 1, :]
     coef[: 8 * strips, :] = jnp.dot(
         inverse, rhs[...], precision=HIGHEST, preferred_element_type=F32
     ).astype(BF16)
@@ -365,8 +406,8 @@
         return pltpu.make_async_remote_copy(
             src_ref=notes.at[lax.rem(me + d, groups)],
             dst_ref=squares.at[d],
-            send_sem=flat.at[6],
-            recv_sem=flat.at[7],
+            send_sem=flat.at[9],
+            recv_sem=flat.at[10],
             device_id=samp_peer(d),
             device_id_type=MESH,
         )
@@ -406,7 +447,7 @@
 
     def scale():
         total = squares[0]
-        await_all(7, squares.at[pl.ds(1, groups - 1)])
+        await_all(10, squares.at[pl.ds(1, groups - 1)])
         for d in range(1, groups):
             total = total + squares[d]
         gain = lax.rsqrt(total / samples + epsilon)
@@ -489,12 +530,22 @@
     ]
     for copy in crossed:
         copy.start()
-    for copy in spread + [swap]:
-        copy.wait_send()
-    await_all(0, landed)
-    await_all(2, landed)
-    await_all(4, gram_landed)
-    await_all(6, squares.at[pl.ds(1, groups - 1)])
+
+    @pl.when(odd == 1)
+    def _():
+        for d in range(1, tiles):
+            spread_copy(d, pair).wait_send()
+        swap.wait_send()
+        await_all(0, landed_t)
+        await_all(2, landed_g.at[0, pl.ds(0, groups - 1)])
+        await_all(5, full.at[0, pl.ds(0, groups - 1)])
+        await_all(7, gram_landed)
+
+    @pl.when(odd == 0)
+    def _():
+        await_all(2, landed_g.at[1])
+
+    await_all(9, squares.at[pl.ds(1, groups - 1)])
     for p in range(n_parts):
         for stage in range(len(areas[p][0])):
             for copy in copies(turns - 1, p, stage):
@@ -524,11 +575,12 @@
             lot //= n
             bufs.append(pltpu.VMEM((turns, n, lot) + size, F32))
             bufs.append(pltpu.VMEM((turns, n - 1, lot) + size, F32))
-    n_blocks = (n_traits // tiles + width) // LANES
-    strips = -(-used // 8)
-    lots = -(-strips // (LANES // (8 * strips) * 2))
-    slots = n_blocks * (used // 8) + -(-n_blocks * (used % 8) // 8)
-    quota = -(-slots // groups)
+    pairs, whole, rest = tiles // 2, used // 8, used % 8
+    n_t, n_g, strips = n_traits // pairs // LANES, width // LANES, -(-used // 8)
+    quota_t = -(-n_t * whole // groups)
+    quota_g = -(-(n_g * whole + -(-(n_t + n_g) * rest // 8)) // groups)
+    quota = quota_t + 2 * quota_g
+    lots = -(-strips // (LANES // (8 * strips)))
     vmem = pl.BlockSpec(memory_space=pltpu.VMEM)
     sems = pltpu.SemaphoreType.DMA((2, len(areas), bits + 1))
     pair = pltpu.SemaphoreType.DMA((2 * tiles - 1,))
@@ -545,12 +597,14 @@
             pltpu.VMEM((used - 1, local), BF16),
             pltpu.VMEM((local, width), jnp.int32),
             pltpu.VMEM((turns - 1, local), jnp.int32),
-            pltpu.SemaphoreType.DMA((4,)),
+            pltpu.SemaphoreType.DMA((10,)),
             pltpu.VMEM((local, LANES), BF16),
-            pltpu.VMEM((quota * groups, 8, LANES), F32),
-            pltpu.VMEM((groups - 1, quota, 8, LANES), F32),
+            pltpu.VMEM((groups * quota_t, 8, LANES), F32),
+            pltpu.VMEM((groups * quota_g, 8, LANES), F32),
+            pltpu.VMEM((groups - 1, quota_t, 8, LANES), F32),
+            pltpu.VMEM((2, groups, quota_g, 8, LANES), F32),
             pltpu.VMEM((quota, 8, LANES), F32),
-            pltpu.VMEM((tiles, quota * groups, 8, LANES), F32),
+            pltpu.VMEM((pairs, groups, quota, 8, LANES), F32),
             pltpu.VMEM((LANES, n_traits + width), F32),
             pltpu.VMEM((LANES, n_traits + width), BF16),
             pltpu.VMEM((n_traits, local), BF16),
@@ -558,16 +612,16 @@
             pltpu.VMEM((local, width + LANES), BF16),
             pltpu.VMEM((turns, own, width), F32),
             pltpu.VMEM((own, width), F32),
-            pltpu.VMEM((2, lots, 8, LANES), F32),
+            pltpu.VMEM((lots, 8, LANES), F32),
             pltpu.VMEM((groups - 1, lots, 8, LANES), F32),
-            pltpu.VMEM((2, lots, 8, LANES), F32),
+            pltpu.VMEM((lots, 8, LANES), F32),
             pltpu.VMEM((LANES // 2, LANES), F32),
             pltpu.VMEM((groups, 8, LANES), F32),
             pltpu.VMEM((groups, 8, LANES), F32),
             pltpu.VMEM((LANES, LANES), F32),
             pltpu.VMEM((8, width), F32),
             pltpu.VMEM((tiles, own, LANES), F32),
-            pltpu.SemaphoreType.DMA((8,)),
+            pltpu.SemaphoreType.DMA((11,)),
             pair,
             pair,
             sems,

time: 80.1 us -> 79 us (0.986)
  Pallas kernels: 78.1 us -> 77 us
    pallas_call x1, Pallas kernels: 78.1 us -> 77 us  [shards(): pl.pallas_call(functools.partial(scan_kernel, groups, tiles, local * grou...]
where the time goes in v4:
time: 79 us; the launch traced here: 78.9 us
  Pallas kernels  77 us (97%)
  local copies, waits for them, and re-layouts  1.22 us (2%)
    pallas_call x1, Pallas kernels, shards(): pl.pallas_call(functools.partial(scan_kernel, groups, tiles, local * grou...  77 us

profile of v4, /device:TPU:0, one launch (start us, length us, event | category | flops | bytes accessed | tf_op | source)
XLA Modules:
  0.0 78.9 jit_solution(1564025003772011146)
XLA Ops:
  0.6 77.0 %scan.1 = (f32[64,256]{1,0:T(8,128)S(1)}, f32[6,64]{1,0:T(8,128)S(1)}) custom-call(bf16[1024,1024]{1,0:T(8,128)(2,1)} %t_hbm.1, bf16[32,1024]{1,0:T(8,128)(2,1)} %bitcast.1, s32[1024,256]{1,0:T(8,128)} %g_hbm.1, s32[6,1024]{1,0:T(8,128)} %order_hbm.1), custom_call_target="tpu_custom_call" | custom-call | tf_op jit(solution)/shard_map/scan/pallas_call | solution.py:587
  77.6 0.6 copy.8
  78.3 0.6 copy.9

commit v5 on v4

--- a/solution.py
+++ b/solution.py
@@ -139,6 +139,8 @@
 
     starts = [sum(2 * len(area[0]) for area in areas[:p]) for p in range(n_parts)]
 
+    places = [sum(len(area[0]) for area in areas[:p]) for p in range(n_parts)]
+
     def source(p, stage):
         return bufs[starts[p] + 2 * stage]
 
@@ -151,11 +153,10 @@
 
     def copies(k, p, stage):
         mine, n, far = digit(p, stage)
-        first = sum(2 ** len(some) - 1 for some in areas[p][0][:stage])
+        at = lax.rem(k, 2), places[p] + stage
         out = []
         for d in range(1, n):
             other = lax.rem(mine + d, n)
-            at = lax.rem(k, 2), p, first + d - 1
             out.append(
                 pltpu.make_async_remote_copy(
                     src_ref=source(p, stage).at[k, other],
@@ -168,6 +169,14 @@
             )
         return out
 
+    def await_stage(k, p, stage, sems, like):
+        sem = sems.at[lax.rem(k, 2), places[p] + stage]
+        pltpu.make_async_copy(like, like, sem).wait()
+
+    def await_sent(k, p, stage):
+        n = digit(p, stage)[1]
+        await_stage(k, p, stage, send, source(p, stage).at[k, pl.ds(0, n - 1)])
+
     def begin(k, part):
         for p in HALVES[part]:
             for copy in copies(k, p, 0):
@@ -177,11 +186,9 @@
         for p in HALVES[part]:
             if stage >= len(areas[p][0]):
                 continue
-            for copy in copies(k, p, stage):
-                copy.wait_recv()
+            await_stage(k, p, stage, recv, target(p, stage).at[k])
             if not first:
-                for copy in copies(k - 1, p, stage):
-                    copy.wait_send()
+                await_sent(k - 1, p, stage)
             mine, n, _ = digit(p, stage)
             total = source(p, stage)[k, mine]
             for d in range(1, n):
@@ -548,8 +555,7 @@
     await_all(9, squares.at[pl.ds(1, groups - 1)])
     for p in range(n_parts):
         for stage in range(len(areas[p][0])):
-            for copy in copies(turns - 1, p, stage):
-                copy.wait_send()
+            await_sent(turns - 1, p, stage)
     top = peaks[0]
     for d in range(1, tiles):
         crossed[d - 1].wait()
@@ -582,7 +588,7 @@
     quota = quota_t + 2 * quota_g
     lots = -(-strips // (LANES // (8 * strips)))
     vmem = pl.BlockSpec(memory_space=pltpu.VMEM)
-    sems = pltpu.SemaphoreType.DMA((2, len(areas), bits + 1))
+    sems = pltpu.SemaphoreType.DMA((2, sum(len(area[0]) for area in areas)))
     pair = pltpu.SemaphoreType.DMA((2 * tiles - 1,))
     return pl.pallas_call(
         functools.partial(scan_kernel, groups, tiles, local * groups, used, areas),

time: 79 us -> 78.6 us (level)
  no operation moved by 1% of the time
where the time goes in v5:
time: 78.6 us; the launch traced here: 78.5 us
  Pallas kernels  76.6 us (97%)
  local copies, waits for them, and re-layouts  1.22 us (2%)
    pallas_call x1, Pallas kernels, shards(): pl.pallas_call(functools.partial(scan_kernel, groups, tiles, local * grou...  76.6 us

profile of v5, /device:TPU:0, one launch (start us, length us, event | category | flops | bytes accessed | tf_op | source)
XLA Modules:
  0.0 78.5 jit_solution(6455938912722518923)
XLA Ops:
  0.6 76.6 %scan.1 = (f32[64,256]{1,0:T(8,128)S(1)}, f32[6,64]{1,0:T(8,128)S(1)}) custom-call(bf16[1024,1024]{1,0:T(8,128)(2,1)} %t_hbm.1, bf16[32,1024]{1,0:T(8,128)(2,1)} %bitcast.1, s32[1024,256]{1,0:T(8,128)} %g_hbm.1, s32[6,1024]{1,0:T(8,128)} %order_hbm.1), custom_call_target="tpu_custom_call" | custom-call | tf_op jit(solution)/shard_map/scan/pallas_call | solution.py:593
  77.3 0.6 copy.8
  77.9 0.6 copy.9

commit v6 on v5

--- a/solution.py
+++ b/solution.py
@@ -24,8 +24,8 @@
     return (
         (x_first, slice(0, mid), slice(0, half)),
         (y_first, slice(0, mid), slice(half, width)),
-        (ones[2:] + ones[:2], slice(cut, own), slice(0, half)),
-        (ones[2::-1] + ones[3:], slice(cut, own), slice(half, width)),
+        (ones[2:] + ones[1::-1], slice(cut, own), slice(0, half)),
+        ((ones[2],) + ones[:2] + ones[3:], slice(cut, own), slice(half, width)),
         (x_first, slice(mid, cut), slice(0, half)),
         (y_first, slice(mid, cut), slice(half, width)),
     )
@@ -389,8 +389,6 @@
     cross(1, resid.astype(BF16))
     begin(1, 0)
     begin(1, 1)
-    advance(0, 0, 2, True)
-    advance(0, 1, 2, True)
     sq_g = jnp.zeros((1, width), F32)
     for i in range(local // step):
         at = slice(i * step, (i + 1) * step)
@@ -399,6 +397,9 @@
         )
         sq_g = sq_g + jnp.sum(resid * resid, axis=0, keepdims=True)
         rg[at, :] = resid.astype(BF16)
+
+    advance(0, 0, 2, True)
+    advance(0, 1, 2, True)
 
     def note_squares():
         for j in range(groups):

time: 78.6 us -> 78.6 us (level)
  no operation moved by 1% of the time
where the time goes in v6:
time: 78.6 us; the launch traced here: 78.4 us
  Pallas kernels  76.6 us (97%)
  local copies, waits for them, and re-layouts  1.22 us (2%)
    pallas_call x1, Pallas kernels, shards(): pl.pallas_call(functools.partial(scan_kernel, groups, tiles, local * grou...  76.6 us

profile of v6, /device:TPU:0, one launch (start us, length us, event | category | flops | bytes accessed | tf_op | source)
XLA Modules:
  0.0 78.4 jit_solution(13012837751720738855)
XLA Ops:
  0.6 76.6 %scan.1 = (f32[64,256]{1,0:T(8,128)S(1)}, f32[6,64]{1,0:T(8,128)S(1)}) custom-call(bf16[1024,1024]{1,0:T(8,128)(2,1)} %t_hbm.1, bf16[32,1024]{1,0:T(8,128)(2,1)} %bitcast.1, s32[1024,256]{1,0:T(8,128)} %g_hbm.1, s32[6,1024]{1,0:T(8,128)} %order_hbm.1), custom_call_target="tpu_custom_call" | custom-call | tf_op jit(solution)/shard_map/scan/pallas_call | solution.py:594
  77.2 0.6 copy.8
  77.8 0.6 copy.9
